TPU v7x, 32 devices: a whole 2x2x4 slice. The times are simulated.
32 devices in a mesh: rep: 2 (over x), stretch: 2 (over core), tp: 8 (over z, y).
Axes of the slice: x: 2, y: 2, z: 4, core: 2. Of those that a mesh axis runs over, the one named last changes fastest.
Arguments:
- query: bfloat16 [4, 512, 3072], P(('rep', 'stretch'), 'tp'), parts along dimension 0, may hold values from -64 to 64
- stretch_kv: bfloat16 [2, 4, 512, 3072], P(None, ('rep', 'stretch'), 'tp'), parts along dimension 1, may hold values from -6 to 6
- history_kv: bfloat16 [2, 4096, 3072], P(None, ('rep', 'tp')), parts along dimension 1, may hold values from -6 to 6
- block_mask: int32 [4, 4, 8], P(('rep', 'stretch')), parts along dimension 0, may hold values from 0 to 1, as said below
- noise_level: int32 [4], P(('rep', 'stretch')), parts along dimension 0, may hold values from 0 to 999
- history_blocks: int32 [2], P('rep'), parts along dimension 0, may hold values from 1 to 16
- out_weight: bfloat16 [3072, 6144], P(None, 'tp'), may hold values from -0.109375 to 0.109375
- gate_table: float32 [1000, 6144], P(None, 'tp'), may hold values from -6 to 6
Outputs:
- mixed: bfloat16 [4, 512, 6144], P(('rep', 'stretch'), None, 'tp'), parts along dimension 0
There are 2 independent parts, one for each index of `rep`. A program takes and returns all parts, laid end to end along the dimension named above; an argument that names none is the same for every part. Nothing has to cross between parts.
Inputs may be any that keep to these rules, and one draw needn't show every extreme that they name: block_mask[c, i, 4 + i] = 1 for every query block i; block_mask[0, i, j] = 0 for j < 4.
All inputs are finite; a program needn't handle non-finite values.
Results may differ from a plain program's by a relative error of at most 0.0049.
Values may be sent and summed in bfloat16 or wider, within the bound.
A program may use at most 128 MiB of HBM per device.

v0:
```python
import functools
import math

import jax
import jax.numpy as jnp
from jax import lax
from jax.experimental import pallas as pl
from jax.experimental.pallas import tpu as pltpu
from jax.sharding import PartitionSpec as P

H = 24
HD = 128
BLK = 128


NEGATIVE = -1e30


def shifted(value, axis, steps):
    count = lax.axis_size(axis)
    first, last = (max(0, -steps), min(count, count - steps))
    return lax.ppermute(value, axis, [(source, source + steps) for source in range(first, last)])


def head_block(queries, key_rows, value_rows, allowed):
    key_count = key_rows.shape[0]
    head_count = queries.shape[1]
    key_heads = key_rows.reshape(key_count, head_count, HD)
    scores = jnp.einsum("qhd,khd->qhk", queries, key_heads, preferred_element_type=jnp.float32) * (
        1.0 / math.sqrt(HD)
    )
    scores = jnp.where(allowed[:, None, :], scores, NEGATIVE)
    row_peak = jnp.max(scores, axis=2)
    weights = jnp.where(allowed[:, None, :], jnp.exp(scores - row_peak[:, :, None]), 0.0)
    weight_sum = jnp.sum(weights, axis=2)
    output = None
    value_heads = value_rows.reshape(key_count, head_count, HD).astype(jnp.float32)
    output = jnp.einsum("qhk,khd->qhd", weights, value_heads, precision=lax.Precision.HIGHEST)
    return (row_peak, weight_sum, output)


def combine(earlier, later):
    row_peak = jnp.maximum(earlier[0], later[0])
    scale_one = jnp.exp(earlier[0] - row_peak)
    scale_two = jnp.exp(later[0] - row_peak)
    weight_sum = earlier[1] * scale_one + later[1] * scale_two
    output = None
    output = earlier[2] * scale_one[:, :, None] + later[2] * scale_two[:, :, None]
    return (row_peak, weight_sum, output)


def column_table(columns, block_count):
    return (columns[:, None] == jnp.arange(2 * block_count, dtype=jnp.int32)[None, :]).astype(
        jnp.float32
    )


def attend_all(
    queries,
    query_positions,
    fresh_keys,
    fresh_values,
    fresh_hot,
    mask_table,
    history_pair,
    history_live,
    span,
):
    row_count = queries.shape[0]
    head_count = queries.shape[1]
    block_count = mask_table.shape[0]
    query_hot = (
        (query_positions // BLK)[:, None] == jnp.arange(block_count, dtype=jnp.int32)[None, :]
    ).astype(jnp.float32)
    fresh_allowed = jnp.dot(jnp.dot(query_hot, mask_table), fresh_hot.T) > 0.5
    base_peak = jnp.full((row_count, head_count), NEGATIVE, jnp.float32)
    skipped = (
        base_peak,
        jnp.zeros((row_count, head_count), jnp.float32),
        jnp.zeros((row_count, head_count, HD), jnp.float32),
    )
    result = head_block(queries, fresh_keys, fresh_values, fresh_allowed)
    for sub_block in range(history_pair.shape[1] // span):
        lower_row = sub_block * span
        key_rows = history_pair[0, lower_row : lower_row + span]
        value_rows = history_pair[1, lower_row : lower_row + span]
        live_rows = history_live[lower_row : lower_row + span]
        allowed = jnp.broadcast_to(live_rows[None, :], (row_count, span))
        block_part = lax.cond(
            jnp.any(live_rows),
            lambda: head_block(queries, key_rows, value_rows, allowed),
            lambda: skipped,
        )
        result = combine(result, block_part)
    return result


def on_device(
    query, stretch_kv, history_kv, block_mask, noise_level, history_blocks, out_weight, gate_table
):
    tp_count = lax.axis_size("tp")
    tp_index = lax.axis_index("tp")
    local_rows = query.shape[1]
    feature_width = query.shape[2]
    history_rows = history_kv.shape[1]
    block_count = block_mask.shape[1]
    own_pair = stretch_kv[:, 0]
    older_pair = shifted(own_pair, "stretch", 1)
    mask_table = block_mask[0].astype(jnp.float32)
    live_limit = history_blocks[0] * BLK
    fresh_keys = jnp.concatenate([older_pair[0], own_pair[0]], 0)
    fresh_values = jnp.concatenate([older_pair[1], own_pair[1]], 0)
    own_positions = tp_index * local_rows + jnp.arange(local_rows, dtype=jnp.int32)
    fresh_hot = column_table(
        jnp.concatenate([own_positions // BLK, block_count + own_positions // BLK], 0), block_count
    )
    history_positions = tp_index * history_rows + jnp.arange(history_rows, dtype=jnp.int32)
    history_live = history_positions < live_limit
    piece = lax.all_gather(query[0], "tp", axis=0, tiled=True)
    row_count = piece.shape[0]
    positions = jnp.arange(row_count, dtype=jnp.int32)
    row_peak, weight_sum, output = attend_all(
        piece.reshape(row_count, H, HD),
        positions,
        fresh_keys,
        fresh_values,
        fresh_hot,
        mask_table,
        history_kv,
        history_live,
        BLK,
    )
    got_outputs, got_peaks, got_sums = (
        lax.all_to_all(
            output.reshape(tp_count, local_rows, H, HD),
            "tp",
            split_axis=0,
            concat_axis=0,
            tiled=True,
        ),
        lax.all_to_all(
            row_peak.reshape(tp_count, local_rows, H), "tp", split_axis=0, concat_axis=0, tiled=True
        ),
        lax.all_to_all(
            weight_sum.reshape(tp_count, local_rows, H),
            "tp",
            split_axis=0,
            concat_axis=0,
            tiled=True,
        ),
    )
    overall = jnp.max(got_peaks, axis=0)
    factor = jnp.exp(got_peaks - overall[None])
    merged_sum = jnp.sum(got_sums * factor, axis=0)
    merged = jnp.sum(got_outputs * factor[:, :, :, None], axis=0) / merged_sum[:, :, None]
    attended = merged.reshape(local_rows, feature_width).astype(jnp.bfloat16)
    projected = jnp.dot(
        lax.all_gather(attended, "tp", axis=0, tiled=True),
        out_weight,
        preferred_element_type=jnp.float32,
    )
    level_hot = (jnp.arange(gate_table.shape[0], dtype=jnp.int32) == noise_level[0]).astype(
        jnp.float32
    )[None, :]
    gate_row = jnp.dot(level_hot, gate_table, precision=lax.Precision.HIGHEST)
    return (projected * gate_row).astype(jnp.bfloat16)[None]


MESH = pl.DeviceIdType.MESH
WINDOW = 4
PIECES = 2
LAG = 0


def exchange_order(n):
    far, near = list(range(n // 2, n)), list(range(1, n // 2))
    order = []
    for place, code in enumerate(far):
        order += [code] + near[place : place + 1]
    return order


def crossed(me, code, n):
    partner, bit = 0, 1
    while bit < n:
        digit = lax.rem(me // bit, 2)
        partner = partner + bit * (1 - digit if code & bit else digit)
        bit *= 2
    return partner


def fused_kernel(
    n,
    heads,
    mask_ref,
    blocks_ref,
    query_in,
    fresh_in,
    history_in,
    weight_in,
    gate_ref,
    out_ref,
    kv,
    queries,
    gathered,
    weight,
    bias,
    total,
    in_send,
    in_recv,
    pass_send,
    pass_recv,
    gather_send,
    gather_recv,
    local_sem,
):
    me = lax.axis_index("tp")
    core = lax.axis_index("stretch")
    partner = {"stretch": 1 - core}
    line = n // 2
    spot, side = me // 2, me % 2
    local_rows = query_in.shape[1]
    history_rows = history_in.shape[1]
    row_count = n * local_rows
    history_total = n * history_rows
    other_base = history_total
    own_base = history_total + row_count
    block_count = mask_ref.shape[1]
    piece_blocks = block_count // PIECES
    piece_rows = piece_blocks * BLK

    barrier = pltpu.get_barrier_semaphore()
    for offset in range(1, n):
        pl.semaphore_signal(
            barrier, inc=1, device_id={"tp": lax.rem(me + offset, n)}, device_id_type=MESH
        )
    pl.semaphore_signal(barrier, inc=1, device_id=partner, device_id_type=MESH)
    pl.semaphore_wait(barrier, n)

    def remote(source, target, send, recv, device):
        return pltpu.make_async_remote_copy(
            src_ref=source,
            dst_ref=target,
            send_sem=send,
            recv_sem=recv,
            device_id=device,
            device_id_type=MESH,
        )

    def columns(owner, head):
        return pl.ds(pl.multiple_of((owner * heads + head) * HD, HD), HD)

    def history_span(source):
        return pl.ds(pl.multiple_of(source * history_rows, history_rows), history_rows)

    def fresh_span(base, source):
        return pl.ds(pl.multiple_of(base + source * local_rows, local_rows), local_rows)

    def inbound(head, source, target):
        wide = columns(target, head)
        device = {"tp": target}
        return (
            remote(
                history_in.at[core, :, wide],
                kv.at[head, core, history_span(source), :],
                in_send.at[0, head, target],
                in_recv.at[0, head, source],
                device,
            ),
            remote(
                fresh_in.at[:, 0, :, wide],
                kv.at[head, :, fresh_span(own_base, source), :],
                in_send.at[1, head, target],
                in_recv.at[1, head, source],
                device,
            ),
            remote(
                query_in.at[0, :, wide],
                queries.at[head, fresh_span(0, source), :],
                in_send.at[2, head, target],
                in_recv.at[2, head, source],
                device,
            ),
        )

    def passed_history(head, source, which):
        place = kv.at[head, which, history_span(source), :]
        return remote(
            place, place, pass_send.at[0, head, source], pass_recv.at[0, head, source], partner
        )

    def passed_fresh(head, source):
        return remote(
            kv.at[head, :, fresh_span(own_base, source), :],
            kv.at[head, :, fresh_span(other_base, source), :],
            pass_send.at[1, head, source],
            pass_recv.at[1, head, source],
            partner,
        )

    def own_fresh(head):
        return remote(
            fresh_in.at[:, 0, :, columns(me, head)],
            kv.at[head, :, fresh_span(other_base, me), :],
            pass_send.at[1, head, me],
            pass_recv.at[1, head, me],
            partner,
        )

    def local_copy(head, place):
        wide = columns(me, head)
        source, target = (
            (history_in.at[:, :, wide], kv.at[head, :, history_span(me), :]),
            (fresh_in.at[:, 0, :, wide], kv.at[head, :, fresh_span(own_base, me), :]),
            (query_in.at[0, :, wide], queries.at[head, fresh_span(0, me), :]),
            (weight_in.at[:, head], weight.at[head]),
        )[place]
        return pltpu.make_async_copy(source, target, local_sem.at[place, head])

    peers = [crossed(me, code, n) for code in exchange_order(n)]
    steps = [(head, peer) for head in range(heads) for peer in peers]

    def send_step(index):
        if index < len(steps):
            head, peer = steps[index]
            for copy in inbound(head, me, peer):
                copy.start()

    for index in range(WINDOW):
        send_step(index)
    for head in range(heads):
        own_fresh(head).start()
        for place in range(4):
            local_copy(head, place).start()

    live = blocks_ref[0] * BLK
    positions = lax.broadcasted_iota(jnp.int32, (1, history_total), 1)
    history_bias = jnp.where(positions < live, 0.0, NEGATIVE)
    for block in range(block_count):
        bias[block : block + 1, 0:history_total] = history_bias
        for column in range(2 * block_count):
            shown = jnp.full((1, BLK), mask_ref[0, block, column], jnp.int32)
            begin = history_total + column * BLK
            bias[block : block + 1, begin : begin + BLK] = jnp.where(shown > 0, 0.0, NEGATIVE)

    unit = math.log2(math.e) / math.sqrt(HD)

    def attend(head, piece):
        def step(block, carry):
            rows = pl.ds(pl.multiple_of(block * BLK, BLK), BLK)
            scores = lax.dot_general(
                queries[head, rows, :],
                kv[head, 0],
                (((1,), (1,)), ((), ())),
                preferred_element_type=jnp.float32,
            )
            scores = scores * unit + bias[pl.ds(block, 1), :]
            peak = jnp.max(scores, axis=1, keepdims=True)
            weights = jnp.exp2(scores - peak)
            weight_sum = jnp.sum(weights, axis=1, keepdims=True)
            output = jnp.dot(
                weights.astype(jnp.bfloat16), kv[head, 1], preferred_element_type=jnp.float32
            )
            gathered[head, me, rows, :] = (output / weight_sum).astype(jnp.bfloat16)
            return carry

        lax.fori_loop(piece * piece_blocks, (piece + 1) * piece_blocks, step, 0)

    def hop(head, block, way, piece):
        place = gathered.at[head, block, piece * piece_rows : (piece + 1) * piece_rows, :]
        target = (me + 2, me - 2, me + 1 - 2 * side)[way]
        return remote(
            place,
            place,
            gather_send.at[way, head, block * PIECES + piece],
            gather_recv.at[head, block * PIECES + piece],
            {"tp": target},
        )

    def launch(head, block, up, down, piece):
        if up:
            pl.when(spot < line - 1)(lambda: hop(head, block, 0, piece).start())
        if down:
            pl.when(spot > 0)(lambda: hop(head, block, 1, piece).start())
        hop(head, block, 2, piece).start()

    def relay(head, far, piece):
        @pl.when(spot >= far)
        def _():
            block = me - 2 * far
            hop(head, block, 2, piece).wait_recv()
            launch(head, block, True, False, piece)

        @pl.when(spot + far < line)
        def _():
            block = me + 2 * far
            hop(head, block, 2, piece).wait_recv()
            launch(head, block, False, True, piece)

    def finish(head, piece):
        for place in range(line):
            hop(head, 2 * place + 1 - side, 2, piece).wait_recv()

    def project(head, piece):
        last = head == heads - 1

        def step(block, carry):
            rows = pl.ds(pl.multiple_of(block * BLK, BLK), BLK)
            left = jnp.concatenate([gathered[head, source, rows, :] for source in range(n)], axis=1)
            right = weight[head].reshape(n * HD, weight.shape[3])
            part = jnp.dot(left, right, preferred_element_type=jnp.float32)
            if head > 0:
                part = part + total[rows, :]
            if last:
                out_ref[0, rows, :] = (part * gate_ref[...]).astype(out_ref.dtype)
            else:
                total[rows, :] = part
            return carry

        lax.fori_loop(piece * piece_blocks, (piece + 1) * piece_blocks, step, 0)

    relay_after = {len(peers) - 1 - 2 * (line - 1 - LAG - far): far for far in range(1, line - LAG)}
    for head in range(heads):
        for place in range(3):
            local_copy(head, place).wait()
        for place, source in enumerate(peers):
            arrivals = inbound(head, source, me)
            arrivals[0].wait_recv()
            passed_history(head, source, core).start()
            arrivals[1].wait_recv()
            passed_fresh(head, source).start()
            arrivals[2].wait_recv()
            send_step(head * len(peers) + place + WINDOW)
            if head > 0 and place in relay_after:
                for piece in range(PIECES):
                    relay(head - 1, relay_after[place], piece)
        for source in peers:
            passed_history(head, source, 1 - core).wait_recv()
            passed_fresh(head, source).wait_recv()
        own_fresh(head).wait_recv()
        for piece in range(PIECES):
            attend(head, piece)
            launch(head, me, True, True, piece)
        if head > 0:
            if LAG:
                for piece in range(PIECES):
                    relay(head - 1, line - 1, piece)
            local_copy(head - 1, 3).wait()
            for piece in range(PIECES):
                finish(head - 1, piece)
                project(head - 1, piece)
    for far in range(1, line):
        for piece in range(PIECES):
            relay(heads - 1, far, piece)
    local_copy(heads - 1, 3).wait()
    for piece in range(PIECES):
        finish(heads - 1, piece)
        project(heads - 1, piece)

    for head in range(heads):
        for source in peers:
            for copy in inbound(head, me, source):
                copy.wait_send()
            passed_history(head, source, core).wait_send()
            passed_fresh(head, source).wait_send()
        own_fresh(head).wait_send()
        for piece in range(PIECES):

            @pl.when(spot < line - 1)
            def _():
                hop(head, me, 0, piece).wait_send()

            @pl.when(spot > 0)
            def _():
                hop(head, me, 1, piece).wait_send()

            hop(head, me, 2, piece).wait_send()
            for far in range(1, line):

                @pl.when(spot >= far)
                def _():
                    block = me - 2 * far
                    pl.when(spot < line - 1)(lambda: hop(head, block, 0, piece).wait_send())
                    hop(head, block, 2, piece).wait_send()

                @pl.when(spot + far < line)
                def _():
                    block = me + 2 * far
                    pl.when(spot > 0)(lambda: hop(head, block, 1, piece).wait_send())
                    hop(head, block, 2, piece).wait_send()


def on_device_fused(
    query, stretch_kv, history_kv, block_mask, noise_level, history_blocks, out_weight, gate_table
):
    n = lax.axis_size("tp")
    heads = H // n
    local_rows, history_rows = query.shape[1], history_kv.shape[1]
    row_count = n * local_rows
    key_count = n * history_rows + 2 * row_count
    wide = out_weight.shape[1]
    block_count = block_mask.shape[1]
    gate_row = lax.dynamic_slice(gate_table, (noise_level[0], 0), (1, wide))
    anywhere = pl.BlockSpec(memory_space=pl.ANY)
    scalars = pl.BlockSpec(memory_space=pltpu.SMEM)
    vector = pl.BlockSpec(memory_space=pltpu.VMEM)
    dma = pltpu.SemaphoreType.DMA
    return pl.pallas_call(
        functools.partial(fused_kernel, n, heads),
        out_shape=jax.ShapeDtypeStruct((1, row_count, wide), jnp.bfloat16),
        in_specs=[scalars, scalars, anywhere, anywhere, anywhere, anywhere, vector],
        out_specs=vector,
        scratch_shapes=[
            pltpu.VMEM((heads, 2, key_count, HD), jnp.bfloat16),
            pltpu.VMEM((heads, row_count, HD), jnp.bfloat16),
            pltpu.VMEM((heads, n, row_count, HD), jnp.bfloat16),
            pltpu.VMEM((heads, n, HD, wide), jnp.bfloat16),
            pltpu.VMEM((block_count, key_count), jnp.float32),
            pltpu.VMEM((row_count, wide), jnp.float32),
            dma((3, heads, n)),
            dma((3, heads, n)),
            dma((2, heads, n)),
            dma((2, heads, n)),
            dma((3, heads, n * PIECES)),
            dma((heads, n * PIECES)),
            dma((4, heads)),
        ],
        compiler_params=pltpu.CompilerParams(
            collective_id=0, has_side_effects=True, vmem_limit_bytes=60 * 1024 * 1024
        ),
    )(
        block_mask,
        history_blocks,
        query,
        stretch_kv,
        history_kv,
        out_weight.reshape(n, heads, HD, wide),
        gate_row,
    )


def solution(mesh):
    count = mesh.shape["tp"]
    fits = H % count == 0 and count & (count - 1) == 0 and count > 2 and mesh.shape["stretch"] == 2
    return jax.shard_map(
        on_device_fused if fits else on_device,
        mesh=mesh,
        in_specs=(
            P(("rep", "stretch"), "tp", None),
            P(None, ("rep", "stretch"), "tp", None),
            P(None, ("rep", "tp"), None),
            P(("rep", "stretch"), None, None),
            P(("rep", "stretch")),
            P("rep"),
            P(None, "tp"),
            P(None, "tp"),
        ),
        out_specs=P(("rep", "stretch"), None, "tp"),
        check_vma=False,
    )
```

profile of v0, /device:TPU:0, one launch (start us, length us, event | category | flops | bytes accessed | tf_op | source)
XLA Modules:
  0.0 108.9 jit_solution(13170971855007988149)
XLA Ops:
  0.0 0.0 copy-start
  1.6 0.3 copy-done
  1.9 0.6 constant_dynamic-slice_fusion.gate_ref
  2.5 104.3 %shard_map.82 = bf16[1,512,768]{2,1,0:T(8,128)(2,1)} custom-call(s32[1,4,8]{2,1,0:T(4,128)} %mask_ref.1, s32[1]{0:T(128)S(6)} %copy.11.blocks_ref, bf16[1,64,3072]{2,1,0:T(8,128)(2,1)} %query_in.1, bf16[2,1,64,3072]{3,2,1,0:T(8,128)(2,1)} %fresh_in.1, bf16[2,256,3072]{2,1,0:T(8,128)(2,1)} %history_in.1, bf16[8,3,128,768]{3,2,1,0:T(8,128)(2,1)} %bitcast.5, ...), custom_call_target="tpu_custom_call" | custom-call | tf_op jit(solution)/shard_map/pallas_call | solution.py:508
  106.8 2.1 %copy.12 = bf16[1,512,768]{2,1,0:T(8,128)(2,1)} copy(bf16[1,512,768]{2,1,0:T(8,128)(2,1)} %shard_map.82) | data formatting | bytes 1572864
Async XLA Ops:
  0.0 1.9 %copy-start = (f32[1000,768]{1,0:T(8,128)S(1)}, f32[1000,768]{1,0:T(8,128)}, u32[]{:S(2)}) copy-start(f32[1000,768]{1,0:T(8,128)} %param.15) | copy-start | bytes 9216004
where the time goes:
time: 109 us
  Pallas kernels  104 us (95%)
  local copies, waits for them, and re-layouts  2.94 us (3%)
  between operations  1.6 us (1%)
    pallas_call x1, Pallas kernels, on_device_fused(): pl.pallas_call(functools.partial(fused_kernel, n, heads), out_shape=jax.S...  104 us
    unnamed x3, local copies, waits for them, and re-layouts  2.35 us

commit v1 on v0

v1 whole, which is shorter than its diff:
```python
import functools
import math

import jax
import jax.numpy as jnp
from jax import lax
from jax.experimental import pallas as pl
from jax.experimental.pallas import tpu as pltpu
from jax.sharding import PartitionSpec as P

H = 24
HD = 128
BLK = 128


NEGATIVE = -1e30


def shifted(value, axis, steps):
    count = lax.axis_size(axis)
    first, last = (max(0, -steps), min(count, count - steps))
    return lax.ppermute(value, axis, [(source, source + steps) for source in range(first, last)])


def head_block(queries, key_rows, value_rows, allowed):
    key_count = key_rows.shape[0]
    head_count = queries.shape[1]
    key_heads = key_rows.reshape(key_count, head_count, HD)
    scores = jnp.einsum("qhd,khd->qhk", queries, key_heads, preferred_element_type=jnp.float32) * (
        1.0 / math.sqrt(HD)
    )
    scores = jnp.where(allowed[:, None, :], scores, NEGATIVE)
    row_peak = jnp.max(scores, axis=2)
    weights = jnp.where(allowed[:, None, :], jnp.exp(scores - row_peak[:, :, None]), 0.0)
    weight_sum = jnp.sum(weights, axis=2)
    output = None
    value_heads = value_rows.reshape(key_count, head_count, HD).astype(jnp.float32)
    output = jnp.einsum("qhk,khd->qhd", weights, value_heads, precision=lax.Precision.HIGHEST)
    return (row_peak, weight_sum, output)


def combine(earlier, later):
    row_peak = jnp.maximum(earlier[0], later[0])
    scale_one = jnp.exp(earlier[0] - row_peak)
    scale_two = jnp.exp(later[0] - row_peak)
    weight_sum = earlier[1] * scale_one + later[1] * scale_two
    output = None
    output = earlier[2] * scale_one[:, :, None] + later[2] * scale_two[:, :, None]
    return (row_peak, weight_sum, output)


def column_table(columns, block_count):
    return (columns[:, None] == jnp.arange(2 * block_count, dtype=jnp.int32)[None, :]).astype(
        jnp.float32
    )


def attend_all(
    queries,
    query_positions,
    fresh_keys,
    fresh_values,
    fresh_hot,
    mask_table,
    history_pair,
    history_live,
    span,
):
    row_count = queries.shape[0]
    head_count = queries.shape[1]
    block_count = mask_table.shape[0]
    query_hot = (
        (query_positions // BLK)[:, None] == jnp.arange(block_count, dtype=jnp.int32)[None, :]
    ).astype(jnp.float32)
    fresh_allowed = jnp.dot(jnp.dot(query_hot, mask_table), fresh_hot.T) > 0.5
    base_peak = jnp.full((row_count, head_count), NEGATIVE, jnp.float32)
    skipped = (
        base_peak,
        jnp.zeros((row_count, head_count), jnp.float32),
        jnp.zeros((row_count, head_count, HD), jnp.float32),
    )
    result = head_block(queries, fresh_keys, fresh_values, fresh_allowed)
    for sub_block in range(history_pair.shape[1] // span):
        lower_row = sub_block * span
        key_rows = history_pair[0, lower_row : lower_row + span]
        value_rows = history_pair[1, lower_row : lower_row + span]
        live_rows = history_live[lower_row : lower_row + span]
        allowed = jnp.broadcast_to(live_rows[None, :], (row_count, span))
        block_part = lax.cond(
            jnp.any(live_rows),
            lambda: head_block(queries, key_rows, value_rows, allowed),
            lambda: skipped,
        )
        result = combine(result, block_part)
    return result


def on_device(
    query, stretch_kv, history_kv, block_mask, noise_level, history_blocks, out_weight, gate_table
):
    tp_count = lax.axis_size("tp")
    tp_index = lax.axis_index("tp")
    local_rows = query.shape[1]
    feature_width = query.shape[2]
    history_rows = history_kv.shape[1]
    block_count = block_mask.shape[1]
    own_pair = stretch_kv[:, 0]
    older_pair = shifted(own_pair, "stretch", 1)
    mask_table = block_mask[0].astype(jnp.float32)
    live_limit = history_blocks[0] * BLK
    fresh_keys = jnp.concatenate([older_pair[0], own_pair[0]], 0)
    fresh_values = jnp.concatenate([older_pair[1], own_pair[1]], 0)
    own_positions = tp_index * local_rows + jnp.arange(local_rows, dtype=jnp.int32)
    fresh_hot = column_table(
        jnp.concatenate([own_positions // BLK, block_count + own_positions // BLK], 0), block_count
    )
    history_positions = tp_index * history_rows + jnp.arange(history_rows, dtype=jnp.int32)
    history_live = history_positions < live_limit
    piece = lax.all_gather(query[0], "tp", axis=0, tiled=True)
    row_count = piece.shape[0]
    positions = jnp.arange(row_count, dtype=jnp.int32)
    row_peak, weight_sum, output = attend_all(
        piece.reshape(row_count, H, HD),
        positions,
        fresh_keys,
        fresh_values,
        fresh_hot,
        mask_table,
        history_kv,
        history_live,
        BLK,
    )
    got_outputs, got_peaks, got_sums = (
        lax.all_to_all(
            output.reshape(tp_count, local_rows, H, HD),
            "tp",
            split_axis=0,
            concat_axis=0,
            tiled=True,
        ),
        lax.all_to_all(
            row_peak.reshape(tp_count, local_rows, H), "tp", split_axis=0, concat_axis=0, tiled=True
        ),
        lax.all_to_all(
            weight_sum.reshape(tp_count, local_rows, H),
            "tp",
            split_axis=0,
            concat_axis=0,
            tiled=True,
        ),
    )
    overall = jnp.max(got_peaks, axis=0)
    factor = jnp.exp(got_peaks - overall[None])
    merged_sum = jnp.sum(got_sums * factor, axis=0)
    merged = jnp.sum(got_outputs * factor[:, :, :, None], axis=0) / merged_sum[:, :, None]
    attended = merged.reshape(local_rows, feature_width).astype(jnp.bfloat16)
    projected = jnp.dot(
        lax.all_gather(attended, "tp", axis=0, tiled=True),
        out_weight,
        preferred_element_type=jnp.float32,
    )
    level_hot = (jnp.arange(gate_table.shape[0], dtype=jnp.int32) == noise_level[0]).astype(
        jnp.float32
    )[None, :]
    gate_row = jnp.dot(level_hot, gate_table, precision=lax.Precision.HIGHEST)
    return (projected * gate_row).astype(jnp.bfloat16)[None]


MESH = pl.DeviceIdType.MESH
ROWS = (0, 1)
ASKED = (2,)
PIECES = 2
AHEAD = 3
SIDE_AHEAD = 6
THROTTLE = 3
EARLY = 3
COMBINE_LAG = 2
INNER_LAG = 5
RELAY_LAG = 5
OUTER_LAG = 8


def fused_kernel(
    n,
    chunks,
    mask_ref,
    blocks_ref,
    level_ref,
    query_in,
    fresh_in,
    history_in,
    weight_in,
    gate_in,
    out_ref,
    kv,
    queries,
    own_part,
    own_lse,
    part_send,
    part_recv,
    stat_send,
    stat_recv,
    gathered,
    weight,
    gate,
    bias,
    total,
    in_send,
    in_recv,
    fwd_send,
    pass_send,
    pass_recv,
    query_send,
    query_recv,
    swap_send,
    swap_recv,
    gather_send,
    gather_recv,
    local_sem,
    gate_sem,
):
    me = lax.axis_index("tp")
    core = lax.axis_index("stretch")
    twin = {"stretch": 1 - core}
    line = n // 2
    spot, col = me // 2, me % 2
    members = n // 2
    camp = me // members
    seat = me % members
    inner = (spot > 0) & (spot < line - 1)
    mate_spot = spot + 1 - 2 * (spot % 2)
    side_dev = {"tp": me + 1 - 2 * col}
    mate_dev = {"tp": 2 * mate_spot + col}
    mirror_dev = {"tp": 2 * (line - 1 - spot) + col}
    side_seat = seat + 1 - 2 * col
    mate_seat = 2 * (mate_spot % 2) + col
    diagonal_seat = 2 * (mate_spot % 2) + 1 - col

    local_rows = query_in.shape[1]
    history_rows = history_in.shape[1]
    row_count = n * local_rows
    camp_rows = members * local_rows
    camp_history = members * history_rows
    other_base = camp_history
    own_base = camp_history + camp_rows
    block_count = mask_ref.shape[1]
    camp_blocks = block_count // 2
    piece_blocks = block_count // PIECES
    piece_rows = piece_blocks * BLK
    wide = out_ref.shape[2]

    barrier = pltpu.get_barrier_semaphore()
    for offset in range(1, n):
        pl.semaphore_signal(
            barrier, inc=1, device_id={"tp": lax.rem(me + offset, n)}, device_id_type=MESH
        )
    pl.semaphore_signal(barrier, inc=1, device_id=twin, device_id_type=MESH)
    pl.semaphore_wait(barrier, n)

    def remote(source, target, send, recv, device):
        return pltpu.make_async_remote_copy(
            src_ref=source,
            dst_ref=target,
            send_sem=send,
            recv_sem=recv,
            device_id=device,
            device_id_type=MESH,
        )

    def columns(half, j):
        return pl.ds(pl.multiple_of((half * chunks + j) * HD, HD), HD)

    def history_span(source):
        return pl.ds(pl.multiple_of(source * history_rows, history_rows), history_rows)

    def fresh_span(base, source):
        return pl.ds(pl.multiple_of(base + source * local_rows, local_rows), local_rows)

    def query_span(source):
        return pl.ds(
            pl.multiple_of((camp * members + source) * local_rows, local_rows), local_rows
        )

    def places(j, source):
        return (
            kv.at[j, core, history_span(source), :],
            kv.at[j, :, fresh_span(own_base, source), :],
            queries.at[j, query_span(source), :],
        )

    def own_copies(half, j, device, slot, source, kinds):
        cols = columns(half, j)
        origins = (
            history_in.at[core, :, cols],
            fresh_in.at[:, 0, :, cols],
            query_in.at[0, :, cols],
        )
        targets = places(j, source)
        return [
            remote(
                origins[k],
                targets[k],
                in_send.at[k, j, slot],
                in_recv.at[k, j, source],
                device,
            )
            for k in kinds
        ]

    def forward(j, kinds):
        spots = places(j, side_seat)
        return [
            remote(
                spots[k], spots[k], fwd_send.at[k, j], in_recv.at[k, j, side_seat], mate_dev
            )
            for k in kinds
        ]

    def passed_history(j, source, which):
        place = kv.at[j, which, history_span(source), :]
        return remote(
            place, place, pass_send.at[0, j, source], pass_recv.at[0, j, source], twin
        )

    def passed_fresh(j, source):
        return remote(
            kv.at[j, :, fresh_span(own_base, source), :],
            kv.at[j, :, fresh_span(other_base, source), :],
            pass_send.at[1, j, source],
            pass_recv.at[1, j, source],
            twin,
        )

    def own_fresh(j):
        return remote(
            fresh_in.at[:, 0, :, columns(col, j)],
            kv.at[j, :, fresh_span(other_base, seat), :],
            pass_send.at[1, j, seat],
            pass_recv.at[1, j, seat],
            twin,
        )

    def local_copy(j, place):
        cols = columns(col, j)
        source, target = (
            (history_in.at[:, :, cols], kv.at[j, :, history_span(seat), :]),
            (fresh_in.at[:, 0, :, cols], kv.at[j, :, fresh_span(own_base, seat), :]),
            (query_in.at[0, :, cols], queries.at[j, query_span(seat), :]),
            (weight_in.at[:, j], weight.at[j]),
        )[place]
        return pltpu.make_async_copy(source, target, local_sem.at[place, j])

    def mirrored_query(j, which):
        rows = pl.ds(pl.multiple_of(which * camp_rows, camp_rows), camp_rows)
        place = queries.at[j, rows, :]
        return remote(place, place, query_send.at[j], query_recv.at[j], mirror_dev)

    def swapped(j, piece):
        rows = pl.ds(piece * piece_rows, piece_rows)
        return (
            remote(
                part_send.at[j, rows, :],
                part_recv.at[j, rows, :],
                swap_send.at[0, j, piece],
                swap_recv.at[0, j, piece],
                mirror_dev,
            ),
            remote(
                stat_send.at[j, :, rows],
                stat_recv.at[j, :, rows],
                swap_send.at[1, j, piece],
                swap_recv.at[1, j, piece],
                mirror_dev,
            ),
        )

    def spread(half, j, piece):
        place = gathered.at[half * chunks + j, pl.ds(piece * piece_rows, piece_rows), :]
        return [
            remote(
                place,
                place,
                gather_send.at[way, j, piece],
                gather_recv.at[half * chunks + j, piece],
                device,
            )
            for way, device in enumerate((side_dev, mate_dev))
        ]

    def block_rows(block):
        return pl.ds(pl.multiple_of(block * BLK, BLK), BLK)

    gate_copy = pltpu.make_async_copy(gate_in, gate, gate_sem)
    unit = math.log2(math.e) / math.sqrt(HD)

    def prepare_bias():
        live = blocks_ref[0] * BLK
        positions = camp * camp_history + lax.broadcasted_iota(
            jnp.int32, (1, camp_history), 1
        )
        history_bias = jnp.where(positions < live, 0.0, NEGATIVE)
        for block in range(block_count):
            bias[block : block + 1, 0:camp_history] = history_bias
            for part in range(2):
                for near in range(camp_blocks):
                    column = part * block_count + camp * camp_blocks + near
                    shown = jnp.full((1, BLK), mask_ref[0, block, column], jnp.int32)
                    begin = camp_history + part * camp_rows + near * BLK
                    bias[block : block + 1, begin : begin + BLK] = jnp.where(
                        shown > 0, 0.0, NEGATIVE
                    )

    def attend(j, piece):
        rows = pl.ds(piece * piece_rows, piece_rows)
        scores = lax.dot_general(
            queries[j, rows, :],
            kv[j, 0],
            (((1,), (1,)), ((), ())),
            preferred_element_type=jnp.float32,
        )
        peaks, sums, parts = [], [], []
        for place in range(piece_blocks):
            block = piece * piece_blocks + place
            part = scores[place * BLK : (place + 1) * BLK] * unit + bias[block : block + 1, :]
            peak = jnp.max(part, axis=1, keepdims=True)
            part = jnp.exp2(part - peak)
            peaks.append(peak)
            sums.append(jnp.sum(part, axis=1, keepdims=True))
            parts.append(part.astype(jnp.bfloat16))
        output = jnp.dot(
            jnp.concatenate(parts, axis=0), kv[j, 1], preferred_element_type=jnp.float32
        )
        output = output / jnp.concatenate(sums, axis=0)
        own_part[j, rows, :] = output
        part_send[j, rows, :] = output.astype(jnp.bfloat16)
        for place in range(piece_blocks):
            begin = piece * piece_rows + place * BLK
            level = jnp.broadcast_to(peaks[place] + jnp.log2(sums[place]), (BLK, BLK))
            own_lse[j, begin : begin + BLK, :] = level
            stat_send[j, :, begin : begin + BLK] = level.T[0:8, :]

    def combine(j, piece):
        def step(block, carry):
            rows = block_rows(block)
            mine = own_lse[j, rows, :]
            theirs = jnp.broadcast_to(stat_recv[j, 0:1, rows], (BLK, BLK)).T
            top = jnp.maximum(mine, theirs)
            first = jnp.exp2(mine - top)
            second = jnp.exp2(theirs - top)
            mixed = own_part[j, rows, :] * first + part_recv[j, rows, :].astype(
                jnp.float32
            ) * second
            gathered[col * chunks + j, rows, :] = (mixed / (first + second)).astype(
                jnp.bfloat16
            )
            return carry

        lax.fori_loop(piece * piece_blocks, (piece + 1) * piece_blocks, step, 0)

    def project(j, halves, last):
        local_copy(j, 3).wait()
        for piece in range(PIECES):
            for half in halves:
                spread(half, j, piece)[0].wait_recv()

            def step(block, carry):
                rows = block_rows(block)
                left = jnp.concatenate(
                    [gathered[j, rows, :], gathered[chunks + j, rows, :]], axis=1
                )
                right = weight[j].reshape(2 * HD, wide)
                part = jnp.dot(left, right, preferred_element_type=jnp.float32)
                part = part + total[rows, :]
                if last:
                    factor = gate[pl.ds(level_ref[0], 1), :]
                    out_ref[0, rows, :] = (part * factor).astype(out_ref.dtype)
                else:
                    total[rows, :] = part
                return carry

            lax.fori_loop(piece * piece_blocks, (piece + 1) * piece_blocks, step, 0)

    def every(body, count=chunks, first=0):
        def step(j, carry):
            body(j)
            return carry

        lax.fori_loop(first, count, step, 0)

    def start(copies):
        for copy in copies:
            copy.start()

    @pl.when(inner)
    def _():
        def ask(j):
            start(own_copies(1 - col, j, side_dev, 0, seat, ASKED))

        def begin(j):
            start(own_copies(1 - col, j, side_dev, 0, seat, ROWS))
            pl.when(j + EARLY < chunks)(lambda: ask(j + EARLY))

        every(ask, EARLY)
        every(begin, SIDE_AHEAD)

        def fetch(j):
            for place in range(4):
                local_copy(j, place).start()
            own_fresh(j).start()

        every(fetch)
        gate_copy.start()
        total[...] = jnp.zeros_like(total)
        prepare_bias()
        sources = (side_seat, mate_seat, diagonal_seat)

        def answer(j):
            local_copy(j, 2).wait()
            for source in sources:
                own_copies(col, j, side_dev, 0, source, ASKED)[0].wait_recv()
            mirrored_query(j, camp).start()

        every(answer, EARLY)

        def take(j):
            for place in range(2):
                local_copy(j, place).wait()
            for source in sources:
                arrivals = own_copies(col, j, side_dev, 0, source, ROWS)
                arrivals[0].wait_recv()
                passed_history(j, source, core).start()
                arrivals[1].wait_recv()
                passed_fresh(j, source).start()
            pl.when(j + SIDE_AHEAD < chunks)(lambda: begin(j + SIDE_AHEAD))
            pl.when(j + EARLY < chunks)(lambda: answer(j + EARLY))

        def work(j):
            for source in sources:
                passed_history(j, source, 1 - core).wait_recv()
                passed_fresh(j, source).wait_recv()
            own_fresh(j).wait_recv()
            mirrored_query(j, 1 - camp).wait_recv()
            for piece in range(PIECES):
                attend(j, piece)
                start(swapped(j, piece))

        def merge(j):
            for piece in range(PIECES):
                for copy in swapped(j, piece):
                    copy.wait_recv()
                combine(j, piece)
                start(spread(col, j, piece))

        def round_of(step):
            pl.when(step < chunks)(lambda: take(step))
            pl.when((step >= COMBINE_LAG) & (step < chunks + COMBINE_LAG))(
                lambda: merge(step - COMBINE_LAG)
            )
            pl.when(step >= INNER_LAG)(
                lambda: project(step - INNER_LAG, (1 - col,), False)
            )
            pl.when(step < chunks)(lambda: work(step))

        every(round_of, chunks - 1 + INNER_LAG)
        gate_copy.wait()
        project(chunks - 1, (1 - col,), True)

        def drain(j):
            for copy in own_copies(1 - col, j, side_dev, 0, seat, ROWS + ASKED):
                copy.wait_send()
            for source in sources:
                passed_history(j, source, core).wait_send()
                passed_fresh(j, source).wait_send()
            own_fresh(j).wait_send()
            mirrored_query(j, camp).wait_send()
            for piece in range(PIECES):
                for copy in swapped(j, piece):
                    copy.wait_send()
                for copy in spread(col, j, piece):
                    copy.wait_send()

        every(drain)

    @pl.when(jnp.logical_not(inner))
    def _():
        def ask(j):
            start(own_copies(1 - col, j, side_dev, 1, seat, ASKED))
            start(own_copies(col, j, mate_dev, 0, seat, ASKED))

        def begin(j):
            start(own_copies(col, j, mate_dev, 0, seat, ROWS))

        def begin_side(j):
            start(own_copies(1 - col, j, side_dev, 1, seat, ROWS))
            pl.when(j + EARLY < chunks)(lambda: ask(j + EARLY))

        every(ask, EARLY)
        every(begin, AHEAD)
        every(begin_side, SIDE_AHEAD)
        every(lambda j: local_copy(j, 3).start())
        gate_copy.start()
        total[...] = jnp.zeros_like(total)

        def pass_on(j, kinds):
            arrivals = own_copies(col, j, side_dev, 1, side_seat, kinds)
            copies = forward(j, kinds)
            for arrival, copy in zip(arrivals, copies):
                arrival.wait_recv()
                copy.start()

        every(lambda j: pass_on(j, ASKED), EARLY)

        def hand_on(j):
            pass_on(j, ROWS)
            pl.when(j + AHEAD < chunks)(lambda: begin(j + AHEAD))
            pl.when(j + SIDE_AHEAD < chunks)(lambda: begin_side(j + SIDE_AHEAD))
            pl.when(j + EARLY < chunks)(lambda: pass_on(j + EARLY, ASKED))

        def settle(j):
            for copy in forward(j, ROWS + ASKED):
                copy.wait_send()

        def relay(j):
            for piece in range(PIECES):
                copies = spread(col, j, piece)
                copies[0].wait_recv()
                copies[0].start()

        def round_of(step):
            pl.when(step < chunks)(lambda: hand_on(step))
            pl.when((step >= THROTTLE) & (step < chunks + THROTTLE))(
                lambda: settle(step - THROTTLE)
            )
            pl.when((step >= RELAY_LAG) & (step < chunks + RELAY_LAG))(
                lambda: relay(step - RELAY_LAG)
            )
            pl.when(step >= OUTER_LAG)(
                lambda: project(step - OUTER_LAG, (1 - col,), False)
            )

        every(round_of, chunks - 1 + OUTER_LAG)
        gate_copy.wait()
        project(chunks - 1, (1 - col,), True)

        def drain(j):
            for copy in own_copies(col, j, mate_dev, 0, seat, ROWS + ASKED):
                copy.wait_send()
            for copy in own_copies(1 - col, j, side_dev, 1, seat, ROWS + ASKED):
                copy.wait_send()
            for piece in range(PIECES):
                spread(col, j, piece)[0].wait_send()

        every(drain)


def on_device_fused(
    query, stretch_kv, history_kv, block_mask, noise_level, history_blocks, out_weight, gate_table
):
    n = lax.axis_size("tp")
    chunks = H // 2
    local_rows, history_rows = query.shape[1], history_kv.shape[1]
    row_count = n * local_rows
    key_count = (n * history_rows + 2 * row_count) // 2
    wide = out_weight.shape[1]
    block_count = block_mask.shape[1]
    anywhere = pl.BlockSpec(memory_space=pl.ANY)
    scalars = pl.BlockSpec(memory_space=pltpu.SMEM)
    vector = pl.BlockSpec(memory_space=pltpu.VMEM)
    dma = pltpu.SemaphoreType.DMA
    return pl.pallas_call(
        functools.partial(fused_kernel, n, chunks),
        out_shape=jax.ShapeDtypeStruct((1, row_count, wide), jnp.bfloat16),
        in_specs=[scalars, scalars, scalars, anywhere, anywhere, anywhere, anywhere, anywhere],
        out_specs=vector,
        scratch_shapes=[
            pltpu.VMEM((chunks, 2, key_count, HD), jnp.bfloat16),
            pltpu.VMEM((chunks, row_count, HD), jnp.bfloat16),
            pltpu.VMEM((chunks, row_count, HD), jnp.float32),
            pltpu.VMEM((chunks, row_count, HD), jnp.float32),
            pltpu.VMEM((chunks, row_count, HD), jnp.bfloat16),
            pltpu.VMEM((chunks, row_count, HD), jnp.bfloat16),
            pltpu.VMEM((chunks, 8, row_count), jnp.float32),
            pltpu.VMEM((chunks, 8, row_count), jnp.float32),
            pltpu.VMEM((2 * chunks, row_count, HD), jnp.bfloat16),
            pltpu.VMEM((chunks, 2, HD, wide), jnp.bfloat16),
            pltpu.VMEM(gate_table.shape, jnp.float32),
            pltpu.VMEM((block_count, key_count), jnp.float32),
            pltpu.VMEM((row_count, wide), jnp.float32),
            dma((3, chunks, 2)),
            dma((3, chunks, n // 2)),
            dma((3, chunks)),
            dma((2, chunks, n // 2)),
            dma((2, chunks, n // 2)),
            dma((chunks,)),
            dma((chunks,)),
            dma((2, chunks, PIECES)),
            dma((2, chunks, PIECES)),
            dma((2, chunks, PIECES)),
            dma((2 * chunks, PIECES)),
            dma((4, chunks)),
            dma,
        ],
        compiler_params=pltpu.CompilerParams(
            collective_id=0, has_side_effects=True, vmem_limit_bytes=63 * 1024 * 1024
        ),
    )(
        block_mask,
        history_blocks,
        noise_level,
        query,
        stretch_kv,
        history_kv,
        out_weight.reshape(2, chunks, HD, wide),
        gate_table,
    )


def solution(mesh):
    count = mesh.shape["tp"]
    fits = H % 2 == 0 and count // 2 == 4 and count % 2 == 0 and mesh.shape["stretch"] == 2
    return jax.shard_map(
        on_device_fused if fits else on_device,
        mesh=mesh,
        in_specs=(
            P(("rep", "stretch"), "tp", None),
            P(None, ("rep", "stretch"), "tp", None),
            P(None, ("rep", "tp"), None),
            P(("rep", "stretch"), None, None),
            P(("rep", "stretch")),
            P("rep"),
            P(None, "tp"),
            P(None, "tp"),
        ),
        out_specs=P(("rep", "stretch"), None, "tp"),
        check_vma=False,
    )
```

time: 109 us -> 97.8 us (0.90)
  Pallas kernels: 104 us -> 94.2 us
    pallas_call x1, Pallas kernels: 104 us -> 94.2 us  [on_device_fused(): pl.pallas_call(functools.partial(fused_kernel, n, chunks), out_shape=jax....]
    unnamed x3 -> x1, local copies, waits for them, and re-layouts: 2.35 us -> 2.06 us
where the time goes in v1:
time: 97.8 us; the launch traced here: 97.6 us
  Pallas kernels  94.2 us (96%)
  local copies, waits for them, and re-layouts  2.06 us (2%)
  between operations  1.3 us (1%)
    pallas_call x1, Pallas kernels, on_device_fused(): pl.pallas_call(functools.partial(fused_kernel, n, chunks), out_shape=jax....  94.2 us
    unnamed x1, local copies, waits for them, and re-layouts  2.06 us

profile of v1, /device:TPU:0, one launch (start us, length us, event | category | flops | bytes accessed | tf_op | source)
XLA Modules:
  0.0 97.6 jit_solution(11857700154372773020)
XLA Ops:
  1.3 94.2 %shard_map.82 = bf16[1,512,768]{2,1,0:T(8,128)(2,1)} custom-call(s32[1,4,8]{2,1,0:T(4,128)} %mask_ref.1, s32[1]{0:T(128)S(6)} %copy.11.blocks_ref, s32[1]{0:T(128)S(6)} %copy.10.level_ref, bf16[1,64,3072]{2,1,0:T(8,128)(2,1)} %query_in.1, bf16[2,1,64,3072]{3,2,1,0:T(8,128)(2,1)} %fresh_in.1, bf16[2,256,3072]{2,1,0:T(8,128)(2,1)} %history_in.1, ...), custom_call_target="tpu_custom_call" | custom-call | tf_op jit(solution)/shard_map/pallas_call | solution.py:670
  95.5 2.1 %copy.12 = bf16[1,512,768]{2,1,0:T(8,128)(2,1)} copy(bf16[1,512,768]{2,1,0:T(8,128)(2,1)} %shard_map.82) | data formatting | bytes 1572864

commit v2 on v1

--- a/solution.py
+++ b/solution.py
@@ -207,7 +207,7 @@
     total,
     in_send,
     in_recv,
-    fwd_send,
+    forward_send,
     pass_send,
     pass_recv,
     query_send,
@@ -216,7 +216,7 @@
     swap_recv,
     gather_send,
     gather_recv,
-    local_sem,
+    weight_sem,
     gate_sem,
 ):
     me = lax.axis_index("tp")
@@ -233,8 +233,6 @@
     mate_dev = {"tp": 2 * mate_spot + col}
     mirror_dev = {"tp": 2 * (line - 1 - spot) + col}
     side_seat = seat + 1 - 2 * col
-    mate_seat = 2 * (mate_spot % 2) + col
-    diagonal_seat = 2 * (mate_spot % 2) + 1 - col
 
     local_rows = query_in.shape[1]
     history_rows = history_in.shape[1]
@@ -281,6 +279,9 @@
             pl.multiple_of((camp * members + source) * local_rows, local_rows), local_rows
         )
 
+    camp_span = pl.ds(pl.multiple_of(camp * camp_rows, camp_rows), camp_rows)
+    far_span = pl.ds(pl.multiple_of((1 - camp) * camp_rows, camp_rows), camp_rows)
+
     def places(j, source):
         return (
             kv.at[j, core, history_span(source), :],
@@ -288,72 +289,60 @@
             queries.at[j, query_span(source), :],
         )
 
-    def own_copies(half, j, device, slot, source, kinds):
+    def wholes(j):
+        return (
+            kv.at[j, core, 0:camp_history, :],
+            kv.at[j, :, own_base : own_base + camp_rows, :],
+            queries.at[j, camp_span, :],
+        )
+
+    def origins(half, j):
         cols = columns(half, j)
-        origins = (
+        return (
             history_in.at[core, :, cols],
             fresh_in.at[:, 0, :, cols],
             query_in.at[0, :, cols],
         )
-        targets = places(j, source)
+
+    def own_copies(half, j, device, slot, source, kinds):
+        from_refs, to_refs = origins(half, j), places(j, source)
         return [
-            remote(
-                origins[k],
-                targets[k],
-                in_send.at[k, j, slot],
-                in_recv.at[k, j, source],
-                device,
-            )
+            remote(from_refs[k], to_refs[k], in_send.at[k, slot], in_recv.at[k, j], device)
             for k in kinds
         ]
 
     def forward(j, kinds):
         spots = places(j, side_seat)
         return [
-            remote(
-                spots[k], spots[k], fwd_send.at[k, j], in_recv.at[k, j, side_seat], mate_dev
-            )
+            remote(spots[k], spots[k], forward_send.at[k, j], in_recv.at[k, j], mate_dev)
             for k in kinds
         ]
 
-    def passed_history(j, source, which):
-        place = kv.at[j, which, history_span(source), :]
+    def local_copies(j):
+        from_refs, to_refs = origins(col, j), places(j, seat)
+        return [
+            pltpu.make_async_copy(from_refs[k], to_refs[k], in_recv.at[k, j]) for k in range(3)
+        ]
+
+    def await_bytes(ref, sem):
+        pltpu.make_async_copy(ref, ref, sem).wait()
+
+    def passed_history(j, which):
+        place = kv.at[j, which, 0:camp_history, :]
+        return remote(place, place, pass_send.at[0], pass_recv.at[0, j], twin)
+
+    def passed_fresh(j):
         return remote(
-            place, place, pass_send.at[0, j, source], pass_recv.at[0, j, source], twin
-        )
-
-    def passed_fresh(j, source):
-        return remote(
-            kv.at[j, :, fresh_span(own_base, source), :],
-            kv.at[j, :, fresh_span(other_base, source), :],
-            pass_send.at[1, j, source],
-            pass_recv.at[1, j, source],
+            kv.at[j, :, own_base : own_base + camp_rows, :],
+            kv.at[j, :, other_base : other_base + camp_rows, :],
+            pass_send.at[1],
+            pass_recv.at[1, j],
             twin,
         )
 
-    def own_fresh(j):
-        return remote(
-            fresh_in.at[:, 0, :, columns(col, j)],
-            kv.at[j, :, fresh_span(other_base, seat), :],
-            pass_send.at[1, j, seat],
-            pass_recv.at[1, j, seat],
-            twin,
-        )
-
-    def local_copy(j, place):
-        cols = columns(col, j)
-        source, target = (
-            (history_in.at[:, :, cols], kv.at[j, :, history_span(seat), :]),
-            (fresh_in.at[:, 0, :, cols], kv.at[j, :, fresh_span(own_base, seat), :]),
-            (query_in.at[0, :, cols], queries.at[j, query_span(seat), :]),
-            (weight_in.at[:, j], weight.at[j]),
-        )[place]
-        return pltpu.make_async_copy(source, target, local_sem.at[place, j])
-
-    def mirrored_query(j, which):
-        rows = pl.ds(pl.multiple_of(which * camp_rows, camp_rows), camp_rows)
-        place = queries.at[j, rows, :]
-        return remote(place, place, query_send.at[j], query_recv.at[j], mirror_dev)
+    def mirrored_query(j, span):
+        place = queries.at[j, span, :]
+        return remote(place, place, query_send, query_recv.at[j], mirror_dev)
 
     def swapped(j, piece):
         rows = pl.ds(piece * piece_rows, piece_rows)
@@ -361,14 +350,14 @@
             remote(
                 part_send.at[j, rows, :],
                 part_recv.at[j, rows, :],
-                swap_send.at[0, j, piece],
+                swap_send.at[0],
                 swap_recv.at[0, j, piece],
                 mirror_dev,
             ),
             remote(
                 stat_send.at[j, :, rows],
                 stat_recv.at[j, :, rows],
-                swap_send.at[1, j, piece],
+                swap_send.at[1],
                 swap_recv.at[1, j, piece],
                 mirror_dev,
             ),
@@ -380,7 +369,7 @@
             remote(
                 place,
                 place,
-                gather_send.at[way, j, piece],
+                gather_send.at[way],
                 gather_recv.at[half * chunks + j, piece],
                 device,
             )
@@ -458,7 +447,6 @@
         lax.fori_loop(piece * piece_blocks, (piece + 1) * piece_blocks, step, 0)
 
     def project(j, halves, last):
-        local_copy(j, 3).wait()
         for piece in range(PIECES):
             for half in halves:
                 spread(half, j, piece)[0].wait_recv()
@@ -468,7 +456,7 @@
                 left = jnp.concatenate(
                     [gathered[j, rows, :], gathered[chunks + j, rows, :]], axis=1
                 )
-                right = weight[j].reshape(2 * HD, wide)
+                right = jnp.concatenate([weight[0, j], weight[1, j]], axis=0)
                 part = jnp.dot(left, right, preferred_element_type=jnp.float32)
                 part = part + total[rows, :]
                 if last:
@@ -491,6 +479,14 @@
         for copy in copies:
             copy.start()
 
+    weight_copy = pltpu.make_async_copy(weight_in, weight, weight_sem)
+    own_half = gathered.at[pl.ds(pl.multiple_of(col * chunks, chunks), chunks)]
+
+    def await_own(slot):
+        await_bytes(kv.at[:, 0, 0:history_rows, :], in_send.at[0, slot])
+        await_bytes(kv.at[:, :, 0:local_rows, :], in_send.at[1, slot])
+        await_bytes(queries.at[:, 0:local_rows, :], in_send.at[2, slot])
+
     @pl.when(inner)
     def _():
         def ask(j):
@@ -502,44 +498,30 @@
 
         every(ask, EARLY)
         every(begin, SIDE_AHEAD)
-
-        def fetch(j):
-            for place in range(4):
-                local_copy(j, place).start()
-            own_fresh(j).start()
-
-        every(fetch)
+        every(lambda j: start(local_copies(j)))
+        weight_copy.start()
         gate_copy.start()
         total[...] = jnp.zeros_like(total)
         prepare_bias()
-        sources = (side_seat, mate_seat, diagonal_seat)
 
         def answer(j):
-            local_copy(j, 2).wait()
-            for source in sources:
-                own_copies(col, j, side_dev, 0, source, ASKED)[0].wait_recv()
-            mirrored_query(j, camp).start()
+            await_bytes(wholes(j)[2], in_recv.at[2, j])
+            mirrored_query(j, camp_span).start()
 
         every(answer, EARLY)
 
         def take(j):
-            for place in range(2):
-                local_copy(j, place).wait()
-            for source in sources:
-                arrivals = own_copies(col, j, side_dev, 0, source, ROWS)
-                arrivals[0].wait_recv()
-                passed_history(j, source, core).start()
-                arrivals[1].wait_recv()
-                passed_fresh(j, source).start()
+            await_bytes(wholes(j)[0], in_recv.at[0, j])
+            passed_history(j, core).start()
+            await_bytes(wholes(j)[1], in_recv.at[1, j])
+            passed_fresh(j).start()
             pl.when(j + SIDE_AHEAD < chunks)(lambda: begin(j + SIDE_AHEAD))
             pl.when(j + EARLY < chunks)(lambda: answer(j + EARLY))
 
         def work(j):
-            for source in sources:
-                passed_history(j, source, 1 - core).wait_recv()
-                passed_fresh(j, source).wait_recv()
-            own_fresh(j).wait_recv()
-            mirrored_query(j, 1 - camp).wait_recv()
+            mirrored_query(j, far_span).wait_recv()
+            passed_history(j, 1 - core).wait_recv()
+            passed_fresh(j).wait_recv()
             for piece in range(PIECES):
                 attend(j, piece)
                 start(swapped(j, piece))
@@ -552,6 +534,7 @@
                 start(spread(col, j, piece))
 
         def round_of(step):
+            pl.when(step == INNER_LAG)(weight_copy.wait)
             pl.when(step < chunks)(lambda: take(step))
             pl.when((step >= COMBINE_LAG) & (step < chunks + COMBINE_LAG))(
                 lambda: merge(step - COMBINE_LAG)
@@ -564,22 +547,14 @@
         every(round_of, chunks - 1 + INNER_LAG)
         gate_copy.wait()
         project(chunks - 1, (1 - col,), True)
-
-        def drain(j):
-            for copy in own_copies(1 - col, j, side_dev, 0, seat, ROWS + ASKED):
-                copy.wait_send()
-            for source in sources:
-                passed_history(j, source, core).wait_send()
-                passed_fresh(j, source).wait_send()
-            own_fresh(j).wait_send()
-            mirrored_query(j, camp).wait_send()
-            for piece in range(PIECES):
-                for copy in swapped(j, piece):
-                    copy.wait_send()
-                for copy in spread(col, j, piece):
-                    copy.wait_send()
-
-        every(drain)
+        await_own(0)
+        await_bytes(kv.at[:, 0, 0:camp_history, :], pass_send.at[0])
+        await_bytes(kv.at[:, :, 0:camp_rows, :], pass_send.at[1])
+        await_bytes(queries.at[:, 0:camp_rows, :], query_send)
+        await_bytes(part_send, swap_send.at[0])
+        await_bytes(stat_send, swap_send.at[1])
+        await_bytes(own_half, gather_send.at[0])
+        await_bytes(own_half, gather_send.at[1])
 
     @pl.when(jnp.logical_not(inner))
     def _():
@@ -597,7 +572,7 @@
         every(ask, EARLY)
         every(begin, AHEAD)
         every(begin_side, SIDE_AHEAD)
-        every(lambda j: local_copy(j, 3).start())
+        weight_copy.start()
         gate_copy.start()
         total[...] = jnp.zeros_like(total)
 
@@ -622,11 +597,12 @@
 
         def relay(j):
             for piece in range(PIECES):
-                copies = spread(col, j, piece)
-                copies[0].wait_recv()
-                copies[0].start()
+                copy = spread(col, j, piece)[0]
+                copy.wait_recv()
+                copy.start()
 
         def round_of(step):
+            pl.when(step == OUTER_LAG)(weight_copy.wait)
             pl.when(step < chunks)(lambda: hand_on(step))
             pl.when((step >= THROTTLE) & (step < chunks + THROTTLE))(
                 lambda: settle(step - THROTTLE)
@@ -641,16 +617,9 @@
         every(round_of, chunks - 1 + OUTER_LAG)
         gate_copy.wait()
         project(chunks - 1, (1 - col,), True)
-
-        def drain(j):
-            for copy in own_copies(col, j, mate_dev, 0, seat, ROWS + ASKED):
-                copy.wait_send()
-            for copy in own_copies(1 - col, j, side_dev, 1, seat, ROWS + ASKED):
-                copy.wait_send()
-            for piece in range(PIECES):
-                spread(col, j, piece)[0].wait_send()
-
-        every(drain)
+        await_own(0)
+        await_own(1)
+        await_bytes(own_half, gather_send.at[0])
 
 
 def on_device_fused(
@@ -682,22 +651,22 @@
             pltpu.VMEM((chunks, 8, row_count), jnp.float32),
             pltpu.VMEM((chunks, 8, row_count), jnp.float32),
             pltpu.VMEM((2 * chunks, row_count, HD), jnp.bfloat16),
-            pltpu.VMEM((chunks, 2, HD, wide), jnp.bfloat16),
+            pltpu.VMEM((2, chunks, HD, wide), jnp.bfloat16),
             pltpu.VMEM(gate_table.shape, jnp.float32),
             pltpu.VMEM((block_count, key_count), jnp.float32),
             pltpu.VMEM((row_count, wide), jnp.float32),
-            dma((3, chunks, 2)),
-            dma((3, chunks, n // 2)),
+            dma((3, 2)),
             dma((3, chunks)),
-            dma((2, chunks, n // 2)),
-            dma((2, chunks, n // 2)),
+            dma((3, chunks)),
+            dma((2,)),
+            dma((2, chunks)),
+            dma,
             dma((chunks,)),
-            dma((chunks,)),
+            dma((2,)),
             dma((2, chunks, PIECES)),
-            dma((2, chunks, PIECES)),
-            dma((2, chunks, PIECES)),
+            dma((2,)),
             dma((2 * chunks, PIECES)),
-            dma((4, chunks)),
+            dma,
             dma,
         ],
         compiler_params=pltpu.CompilerParams(

time: 97.8 us -> 93.5 us (0.956)
  Pallas kernels: 94.2 us -> 89.9 us
    pallas_call x1, Pallas kernels: 94.2 us -> 89.9 us  [on_device_fused(): pl.pallas_call(functools.partial(fused_kernel, n, chunks), out_shape=jax....]
where the time goes in v2:
time: 93.5 us; the launch traced here: 93.3 us
  Pallas kernels  89.9 us (96%)
  local copies, waits for them, and re-layouts  2.06 us (2%)
  between operations  1.3 us (1%)
    pallas_call x1, Pallas kernels, on_device_fused(): pl.pallas_call(functools.partial(fused_kernel, n, chunks), out_shape=jax....  89.9 us
    unnamed x1, local copies, waits for them, and re-layouts  2.06 us

profile of v2, /device:TPU:0, one launch (start us, length us, event | category | flops | bytes accessed | tf_op | source)
XLA Modules:
  0.0 93.3 jit_solution(2345230274854327360)
XLA Ops:
  1.3 89.9 %shard_map.82 = bf16[1,512,768]{2,1,0:T(8,128)(2,1)} custom-call(s32[1,4,8]{2,1,0:T(4,128)} %mask_ref.1, s32[1]{0:T(128)S(6)} %copy.11.blocks_ref, s32[1]{0:T(128)S(6)} %copy.10.level_ref, bf16[1,64,3072]{2,1,0:T(8,128)(2,1)} %query_in.1, bf16[2,1,64,3072]{3,2,1,0:T(8,128)(2,1)} %fresh_in.1, bf16[2,256,3072]{2,1,0:T(8,128)(2,1)} %history_in.1, ...), custom_call_target="tpu_custom_call" | custom-call | tf_op jit(solution)/shard_map/pallas_call | solution.py:639
  91.2 2.1 %copy.12 = bf16[1,512,768]{2,1,0:T(8,128)(2,1)} copy(bf16[1,512,768]{2,1,0:T(8,128)(2,1)} %shard_map.82) | data formatting | bytes 1572864

commit v3 on v2

--- a/solution.py
+++ b/solution.py
@@ -170,10 +170,10 @@
 ROWS = (0, 1)
 ASKED = (2,)
 PIECES = 2
-AHEAD = 3
+AHEAD = 1
 SIDE_AHEAD = 6
-THROTTLE = 3
-EARLY = 3
+THROTTLE = 2
+EARLY = 5
 COMBINE_LAG = 2
 INNER_LAG = 5
 RELAY_LAG = 5
@@ -183,9 +183,9 @@
 def fused_kernel(
     n,
     chunks,
-    mask_ref,
-    blocks_ref,
-    level_ref,
+    mask_in,
+    blocks_in,
+    level_in,
     query_in,
     fresh_in,
     history_in,
@@ -205,6 +205,9 @@
     gate,
     bias,
     total,
+    mask_ref,
+    blocks_ref,
+    level_ref,
     in_send,
     in_recv,
     forward_send,
@@ -218,6 +221,7 @@
     gather_recv,
     weight_sem,
     gate_sem,
+    scalar_sem,
 ):
     me = lax.axis_index("tp")
     core = lax.axis_index("stretch")
@@ -241,7 +245,7 @@
     camp_history = members * history_rows
     other_base = camp_history
     own_base = camp_history + camp_rows
-    block_count = mask_ref.shape[1]
+    block_count = mask_in.shape[1]
     camp_blocks = block_count // 2
     piece_blocks = block_count // PIECES
     piece_rows = piece_blocks * BLK
@@ -480,6 +484,12 @@
             copy.start()
 
     weight_copy = pltpu.make_async_copy(weight_in, weight, weight_sem)
+    scalar_copies = [
+        pltpu.make_async_copy(source, target, scalar_sem.at[place])
+        for place, (source, target) in enumerate(
+            ((mask_in, mask_ref), (blocks_in, blocks_ref), (level_in, level_ref))
+        )
+    ]
     own_half = gathered.at[pl.ds(pl.multiple_of(col * chunks, chunks), chunks)]
 
     def await_own(slot):
@@ -498,10 +508,13 @@
 
         every(ask, EARLY)
         every(begin, SIDE_AHEAD)
+        start(scalar_copies)
         every(lambda j: start(local_copies(j)))
         weight_copy.start()
         gate_copy.start()
         total[...] = jnp.zeros_like(total)
+        for copy in scalar_copies:
+            copy.wait()
         prepare_bias()
 
         def answer(j):
@@ -572,6 +585,7 @@
         every(ask, EARLY)
         every(begin, AHEAD)
         every(begin_side, SIDE_AHEAD)
+        scalar_copies[2].start()
         weight_copy.start()
         gate_copy.start()
         total[...] = jnp.zeros_like(total)
@@ -616,6 +630,7 @@
 
         every(round_of, chunks - 1 + OUTER_LAG)
         gate_copy.wait()
+        scalar_copies[2].wait()
         project(chunks - 1, (1 - col,), True)
         await_own(0)
         await_own(1)
@@ -633,13 +648,12 @@
     wide = out_weight.shape[1]
     block_count = block_mask.shape[1]
     anywhere = pl.BlockSpec(memory_space=pl.ANY)
-    scalars = pl.BlockSpec(memory_space=pltpu.SMEM)
     vector = pl.BlockSpec(memory_space=pltpu.VMEM)
     dma = pltpu.SemaphoreType.DMA
     return pl.pallas_call(
         functools.partial(fused_kernel, n, chunks),
         out_shape=jax.ShapeDtypeStruct((1, row_count, wide), jnp.bfloat16),
-        in_specs=[scalars, scalars, scalars, anywhere, anywhere, anywhere, anywhere, anywhere],
+        in_specs=[anywhere] * 8,
         out_specs=vector,
         scratch_shapes=[
             pltpu.VMEM((chunks, 2, key_count, HD), jnp.bfloat16),
@@ -655,6 +669,9 @@
             pltpu.VMEM(gate_table.shape, jnp.float32),
             pltpu.VMEM((block_count, key_count), jnp.float32),
             pltpu.VMEM((row_count, wide), jnp.float32),
+            pltpu.SMEM(block_mask.shape, jnp.int32),
+            pltpu.SMEM(history_blocks.shape, jnp.int32),
+            pltpu.SMEM(noise_level.shape, jnp.int32),
             dma((3, 2)),
             dma((3, chunks)),
             dma((3, chunks)),
@@ -668,6 +685,7 @@
             dma((2 * chunks, PIECES)),
             dma,
             dma,
+            dma((3,)),
         ],
         compiler_params=pltpu.CompilerParams(
             collective_id=0, has_side_effects=True, vmem_limit_bytes=63 * 1024 * 1024

time: 93.5 us -> 88.2 us (0.943)
  Pallas kernels: 89.9 us -> 84.6 us
    pallas_call x1, Pallas kernels: 89.9 us -> 84.6 us  [on_device_fused(): pl.pallas_call(functools.partial(fused_kernel, n, chunks), out_shape=jax....]
where the time goes in v3:
time: 88.2 us; the launch traced here: 88 us
  Pallas kernels  84.6 us (96%)
  local copies, waits for them, and re-layouts  2.06 us (2%)
  between operations  1.3 us (1%)
    pallas_call x1, Pallas kernels, on_device_fused(): pl.pallas_call(functools.partial(fused_kernel, n, chunks), out_shape=jax....  84.6 us
    unnamed x1, local copies, waits for them, and re-layouts  2.06 us

profile of v3, /device:TPU:0, one launch (start us, length us, event | category | flops | bytes accessed | tf_op | source)
XLA Modules:
  0.0 88.0 jit_solution(2531697131310008501)
XLA Ops:
  1.3 84.6 %shard_map.82 = bf16[1,512,768]{2,1,0:T(8,128)(2,1)} custom-call(s32[1,4,8]{2,1,0:T(4,128)} %mask_in.1, s32[1]{0:T(128)S(6)} %copy.11.blocks_in, s32[1]{0:T(128)S(6)} %copy.10.level_in, bf16[1,64,3072]{2,1,0:T(8,128)(2,1)} %query_in.1, bf16[2,1,64,3072]{3,2,1,0:T(8,128)(2,1)} %fresh_in.1, bf16[2,256,3072]{2,1,0:T(8,128)(2,1)} %history_in.1, ...), custom_call_target="tpu_custom_call" | custom-call | tf_op jit(solution)/shard_map/pallas_call | solution.py:653
  85.9 2.1 %copy.12 = bf16[1,512,768]{2,1,0:T(8,128)(2,1)} copy(bf16[1,512,768]{2,1,0:T(8,128)(2,1)} %shard_map.82) | data formatting | bytes 1572864

commit v4 on v3

--- a/solution.py
+++ b/solution.py
@@ -252,12 +252,14 @@
     wide = out_ref.shape[2]
 
     barrier = pltpu.get_barrier_semaphore()
-    for offset in range(1, n):
-        pl.semaphore_signal(
-            barrier, inc=1, device_id={"tp": lax.rem(me + offset, n)}, device_id_type=MESH
-        )
-    pl.semaphore_signal(barrier, inc=1, device_id=twin, device_id_type=MESH)
-    pl.semaphore_wait(barrier, n)
+
+    def greet(devices):
+        for device in devices:
+            pl.semaphore_signal(barrier, inc=1, device_id=device, device_id_type=MESH)
+
+    greet((side_dev, mate_dev))
+    pl.when(inner)(lambda: greet((mirror_dev, twin)))
+    pl.semaphore_wait(barrier, jnp.where(inner, 4, 2))
 
     def remote(source, target, send, recv, device):
         return pltpu.make_async_remote_copy(
@@ -506,8 +508,9 @@
             start(own_copies(1 - col, j, side_dev, 0, seat, ROWS))
             pl.when(j + EARLY < chunks)(lambda: ask(j + EARLY))
 
-        every(ask, EARLY)
-        every(begin, SIDE_AHEAD)
+        start(own_copies(1 - col, 0, side_dev, 0, seat, ROWS))
+        every(ask, EARLY + 1)
+        every(begin, SIDE_AHEAD, 1)
         start(scalar_copies)
         every(lambda j: start(local_copies(j)))
         weight_copy.start()
@@ -582,9 +585,11 @@
             start(own_copies(1 - col, j, side_dev, 1, seat, ROWS))
             pl.when(j + EARLY < chunks)(lambda: ask(j + EARLY))
 
-        every(ask, EARLY)
-        every(begin, AHEAD)
-        every(begin_side, SIDE_AHEAD)
+        start(own_copies(1 - col, 0, side_dev, 1, seat, ROWS))
+        begin(0)
+        every(ask, EARLY + 1)
+        every(begin, AHEAD, 1)
+        every(begin_side, SIDE_AHEAD, 1)
         scalar_copies[2].start()
         weight_copy.start()
         gate_copy.start()
@@ -647,13 +652,12 @@
     key_count = (n * history_rows + 2 * row_count) // 2
     wide = out_weight.shape[1]
     block_count = block_mask.shape[1]
-    anywhere = pl.BlockSpec(memory_space=pl.ANY)
     vector = pl.BlockSpec(memory_space=pltpu.VMEM)
     dma = pltpu.SemaphoreType.DMA
     return pl.pallas_call(
         functools.partial(fused_kernel, n, chunks),
-        out_shape=jax.ShapeDtypeStruct((1, row_count, wide), jnp.bfloat16),
-        in_specs=[anywhere] * 8,
+        out_shape=pltpu.VMEM((1, row_count, wide), jnp.bfloat16),
+        in_specs=[pl.BlockSpec(memory_space=pltpu.HBM)] * 8,
         out_specs=vector,
         scratch_shapes=[
             pltpu.VMEM((chunks, 2, key_count, HD), jnp.bfloat16),

time: 88.2 us -> 84.8 us (0.961)
  Pallas kernels: 84.6 us -> 82.4 us
  local copies, waits for them, and re-layouts: 2.06 us -> 0.88 us
    pallas_call x1, Pallas kernels: 84.6 us -> 82.4 us  [on_device_fused(): pl.pallas_call(functools.partial(fused_kernel, n, chunks), out_shape=pltp...]
    unnamed x1, local copies, waits for them, and re-layouts: 2.06 us -> 0.88 us
where the time goes in v4:
time: 84.8 us; the launch traced here: 84.6 us
  Pallas kernels  82.4 us (97%)
  between operations  1.3 us (2%)
  local copies, waits for them, and re-layouts  0.88 us (1%)
    pallas_call x1, Pallas kernels, on_device_fused(): pl.pallas_call(functools.partial(fused_kernel, n, chunks), out_shape=pltp...  82.4 us

profile of v4, /device:TPU:0, one launch (start us, length us, event | category | flops | bytes accessed | tf_op | source)
XLA Modules:
  0.0 84.6 jit_solution(9033180761505182961)
XLA Ops:
  1.3 82.4 %shard_map.82 = bf16[1,512,768]{2,1,0:T(8,128)(2,1)S(1)} custom-call(s32[1,4,8]{2,1,0:T(4,128)} %mask_in.1, s32[1]{0:T(128)S(6)} %copy.12.blocks_in, s32[1]{0:T(128)S(6)} %copy.11.level_in, bf16[1,64,3072]{2,1,0:T(8,128)(2,1)} %query_in.1, bf16[2,1,64,3072]{3,2,1,0:T(8,128)(2,1)} %fresh_in.1, bf16[2,256,3072]{2,1,0:T(8,128)(2,1)} %history_in.1, ...), custom_call_target="tpu_custom_call" | custom-call | tf_op jit(solution)/shard_map/pallas_call | solution.py:657
  83.7 0.9 %copy.10 = bf16[1,512,768]{2,1,0:T(8,128)(2,1)} copy(bf16[1,512,768]{2,1,0:T(8,128)(2,1)S(1)} %shard_map.82) | data formatting | bytes 1572864

commit v5 on v4

--- a/solution.py
+++ b/solution.py
@@ -435,8 +435,8 @@
             stat_send[j, :, begin : begin + BLK] = level.T[0:8, :]
 
     def combine(j, piece):
-        def step(block, carry):
-            rows = block_rows(block)
+        for block in range(piece * piece_blocks, (piece + 1) * piece_blocks):
+            rows = pl.ds(block * BLK, BLK)
             mine = own_lse[j, rows, :]
             theirs = jnp.broadcast_to(stat_recv[j, 0:1, rows], (BLK, BLK)).T
             top = jnp.maximum(mine, theirs)
@@ -448,31 +448,24 @@
             gathered[col * chunks + j, rows, :] = (mixed / (first + second)).astype(
                 jnp.bfloat16
             )
-            return carry
-
-        lax.fori_loop(piece * piece_blocks, (piece + 1) * piece_blocks, step, 0)
 
     def project(j, halves, last):
         for piece in range(PIECES):
             for half in halves:
                 spread(half, j, piece)[0].wait_recv()
 
-            def step(block, carry):
-                rows = block_rows(block)
-                left = jnp.concatenate(
-                    [gathered[j, rows, :], gathered[chunks + j, rows, :]], axis=1
-                )
-                right = jnp.concatenate([weight[0, j], weight[1, j]], axis=0)
-                part = jnp.dot(left, right, preferred_element_type=jnp.float32)
-                part = part + total[rows, :]
-                if last:
-                    factor = gate[pl.ds(level_ref[0], 1), :]
-                    out_ref[0, rows, :] = (part * factor).astype(out_ref.dtype)
-                else:
-                    total[rows, :] = part
-                return carry
-
-            lax.fori_loop(piece * piece_blocks, (piece + 1) * piece_blocks, step, 0)
+            rows = pl.ds(piece * piece_rows, piece_rows)
+            left = jnp.concatenate(
+                [gathered[j, rows, :], gathered[chunks + j, rows, :]], axis=1
+            )
+            right = jnp.concatenate([weight[0, j], weight[1, j]], axis=0)
+            part = jnp.dot(left, right, preferred_element_type=jnp.float32)
+            part = part + total[rows, :]
+            if last:
+                factor = gate[pl.ds(level_ref[0], 1), :]
+                out_ref[0, rows, :] = (part * factor).astype(out_ref.dtype)
+            else:
+                total[rows, :] = part
 
     def every(body, count=chunks, first=0):
         def step(j, carry):

time: 84.8 us -> 83.7 us (0.987)
  Pallas kernels: 82.4 us -> 81.4 us
    pallas_call x1, Pallas kernels: 82.4 us -> 81.4 us  [on_device_fused(): pl.pallas_call(functools.partial(fused_kernel, n, chunks), out_shape=pltp...]
where the time goes in v5:
time: 83.7 us; the launch traced here: 83.6 us
  Pallas kernels  81.4 us (97%)
  between operations  1.3 us (2%)
  local copies, waits for them, and re-layouts  0.88 us (1%)
    pallas_call x1, Pallas kernels, on_device_fused(): pl.pallas_call(functools.partial(fused_kernel, n, chunks), out_shape=pltp...  81.4 us

profile of v5, /device:TPU:0, one launch (start us, length us, event | category | flops | bytes accessed | tf_op | source)
XLA Modules:
  0.0 83.6 jit_solution(199312093092879765)
XLA Ops:
  1.3 81.4 %shard_map.82 = bf16[1,512,768]{2,1,0:T(8,128)(2,1)S(1)} custom-call(s32[1,4,8]{2,1,0:T(4,128)} %mask_in.1, s32[1]{0:T(128)S(6)} %copy.12.blocks_in, s32[1]{0:T(128)S(6)} %copy.11.level_in, bf16[1,64,3072]{2,1,0:T(8,128)(2,1)} %query_in.1, bf16[2,1,64,3072]{3,2,1,0:T(8,128)(2,1)} %fresh_in.1, bf16[2,256,3072]{2,1,0:T(8,128)(2,1)} %history_in.1, ...), custom_call_target="tpu_custom_call" | custom-call | tf_op jit(solution)/shard_map/pallas_call | solution.py:650
  82.7 0.9 %copy.10 = bf16[1,512,768]{2,1,0:T(8,128)(2,1)} copy(bf16[1,512,768]{2,1,0:T(8,128)(2,1)S(1)} %shard_map.82) | data formatting | bytes 1572864

commit v6 on v5

--- a/solution.py
+++ b/solution.py
@@ -175,9 +175,9 @@
 THROTTLE = 2
 EARLY = 5
 COMBINE_LAG = 2
-INNER_LAG = 5
+INNER_LAG = 4
 RELAY_LAG = 5
-OUTER_LAG = 8
+OUTER_LAG = 7
 
 
 def fused_kernel(
@@ -250,6 +250,7 @@
     piece_blocks = block_count // PIECES
     piece_rows = piece_blocks * BLK
     wide = out_ref.shape[2]
+    swap_rows = piece_rows + 2 * 8 * piece_rows // HD
 
     barrier = pltpu.get_barrier_semaphore()
 
@@ -357,14 +358,14 @@
                 part_send.at[j, rows, :],
                 part_recv.at[j, rows, :],
                 swap_send.at[0],
-                swap_recv.at[0, j, piece],
+                swap_recv.at[j, piece],
                 mirror_dev,
             ),
             remote(
                 stat_send.at[j, :, rows],
                 stat_recv.at[j, :, rows],
                 swap_send.at[1],
-                swap_recv.at[1, j, piece],
+                swap_recv.at[j, piece],
                 mirror_dev,
             ),
         )
@@ -537,10 +538,9 @@
 
         def merge(j):
             for piece in range(PIECES):
-                for copy in swapped(j, piece):
-                    copy.wait_recv()
+                await_bytes(kv.at[0, 0, 0:swap_rows, :], swap_recv.at[j, piece])
                 combine(j, piece)
-                start(spread(col, j, piece))
+                start(spread(col, j, piece)[::-1])
 
         def round_of(step):
             pl.when(step == INNER_LAG)(weight_copy.wait)
@@ -677,7 +677,7 @@
             dma,
             dma((chunks,)),
             dma((2,)),
-            dma((2, chunks, PIECES)),
+            dma((chunks, PIECES)),
             dma((2,)),
             dma((2 * chunks, PIECES)),
             dma,

time: 83.7 us -> 83.5 us (level)
  no operation moved by 1% of the time
where the time goes in v6:
time: 83.5 us; the launch traced here: 83.3 us
  Pallas kernels  81.2 us (97%)
  between operations  1.3 us (2%)
  local copies, waits for them, and re-layouts  0.88 us (1%)
    pallas_call x1, Pallas kernels, on_device_fused(): pl.pallas_call(functools.partial(fused_kernel, n, chunks), out_shape=pltp...  81.2 us

profile of v6, /device:TPU:0, one launch (start us, length us, event | category | flops | bytes accessed | tf_op | source)
XLA Modules:
  0.0 83.3 jit_solution(10241178137160097125)
XLA Ops:
  1.3 81.2 %shard_map.82 = bf16[1,512,768]{2,1,0:T(8,128)(2,1)S(1)} custom-call(s32[1,4,8]{2,1,0:T(4,128)} %mask_in.1, s32[1]{0:T(128)S(6)} %copy.12.blocks_in, s32[1]{0:T(128)S(6)} %copy.11.level_in, bf16[1,64,3072]{2,1,0:T(8,128)(2,1)} %query_in.1, bf16[2,1,64,3072]{3,2,1,0:T(8,128)(2,1)} %fresh_in.1, bf16[2,256,3072]{2,1,0:T(8,128)(2,1)} %history_in.1, ...), custom_call_target="tpu_custom_call" | custom-call | tf_op jit(solution)/shard_map/pallas_call | solution.py:650
  82.5 0.9 %copy.10 = bf16[1,512,768]{2,1,0:T(8,128)(2,1)} copy(bf16[1,512,768]{2,1,0:T(8,128)(2,1)S(1)} %shard_map.82) | data formatting | bytes 1572864
